TPU v7x, 128 devices: a whole 4x4x4 slice. The times are simulated.
128 devices in a mesh: dp: 32 (over z, y, x_hi), section: 2 (over core), tensor: 2 (over x_lo).
Axes of the slice: x: 4 (x_hi: 2, x_lo: 2; x = x_hi * 2 + x_lo), y: 4, z: 4, core: 2. Of those that a mesh axis runs over, the one named last changes fastest.
Arguments:
- tokens: bfloat16 [512, 32, 1024], P('dp'), may hold values from -6 to 6
- counts: int32 [512], replicated, may hold values from 8 to 32, as said below
- assign: int32 [512], replicated, may hold values from 0 to 511, as said below
- qkv_weight: bfloat16 [2, 1024, 3, 1024], P('section', 'dp', None, 'tensor'), may hold values from -0.9375 to 0.9375
- out_weight: bfloat16 [2, 1024, 1024], P('section', 'dp'), may hold values from -0.1875 to 0.1875
- up_weight: bfloat16 [2, 1024, 4096], P('section', 'dp', 'tensor'), may hold values from -0.1875 to 0.1875
- up_bias: bfloat16 [2, 4096], P('section', 'tensor'), may hold values from -3 to 3
- down_weight: bfloat16 [2, 4096, 1024], P('section', 'tensor', 'dp'), may hold values from -0.09375 to 0.09375
- attn_gain: bfloat16 [2, 1024], P('section'), may hold values from 0.25 to 1.75
- mlp_gain: bfloat16 [2, 1024], P('section'), may hold values from 0.25 to 1.75
- final_gain: bfloat16 [1024], replicated, may hold values from 0.25 to 1.75
Outputs:
- encoded: bfloat16 [512, 32, 1024], P('dp', 'section', 'tensor')
Inputs may be any that keep to these rules, and one draw needn't show every extreme that they name: `counts`: every count is at least 8, and in every draw some image has all 32 slots live. assign is a permutation of the images. Slot j belongs to data group j // 16, so every data group receives 16 images; within one data group's slots the images stand in increasing order. Images of data group g are tokens rows g * 16 to (g + 1) * 16 - 1. No data group hands more than 1 images to one data group (itself included), and in every draw some pair of data groups exchanges exactly 1. Every data group receives some image from the data group half the axis away.
All inputs are finite; a program needn't handle non-finite values.
Results may differ from a plain program's by a relative error of at most 0.024.
The roundings to bfloat16 on the way count: a program that leaves them out, or rounds other values in their place, can miss the bound.
Values may be sent and summed in bfloat16 or wider, within the bound.
No kernel may reach another device: no remote copies, remote signals or barrier semaphores. Data moves between devices by JAX's collectives and lax.ppermute only.
A program may use at most 128 MiB of HBM per device.

v0:
```python
import jax
import jax.numpy as jnp
from jax import lax
from jax.sharding import PartitionSpec as P

MICRO = 4
HEAD_DIM = 64
epsilon = 1e-06


def cut_along(value, dim, size):
    lengths = value.shape
    tiles = value.reshape(*lengths[:dim], size, lengths[dim] // size, *lengths[dim + 1 :])
    return jnp.moveaxis(tiles, dim, 0)


def edges_of(length, count):
    unit = 8 if length >= 8 * count else 1
    return [length // unit * k // count * unit for k in range(1, count)]


def laid_out(tiles, dim):
    lengths = list(tiles.shape[1:])
    lengths[dim] *= tiles.shape[0]
    return jnp.moveaxis(tiles, 0, dim).reshape(lengths)


def cut_exchange(value, axis, pieces, split_dim, concat_dim):
    tiles = cut_along(value, split_dim, lax.axis_size(axis))
    widest = max(range(1, max(2, tiles.ndim - 1)), key=lambda d: tiles.shape[d])
    done = []
    for section in jnp.split(tiles, edges_of(tiles.shape[widest], pieces), axis=widest):
        if section.size:
            done.append(lax.all_to_all(section, axis, split_axis=0, concat_axis=0, tiled=True))
    return laid_out(jnp.concatenate(done, axis=widest), concat_dim)


def rows_first(arrays, axis, dims):
    turned = [jnp.moveaxis(a, dim, 0) for a, dim in zip(arrays, dims)]
    widths = [t[0].size for t in turned]
    both = jnp.concatenate([t.reshape(-1, w) for t, w in zip(turned, widths)], axis=1)
    out = lax.all_gather(both, axis, axis=0, tiled=True)
    tiles = jnp.split(out, [sum(widths[:k]) for k in range(1, len(widths))], axis=1)
    return tuple(
        (
            jnp.moveaxis(b.reshape(-1, *t.shape[1:]), 0, dim)
            for b, t, dim in zip(tiles, turned, dims)
        )
    )


def over_pieces(value, axis):
    return lax.all_gather(value, axis).astype(jnp.float32).sum(0)


def passed_along(value, axis, by):
    size = lax.axis_size(axis)
    return lax.ppermute(value, axis, [(i, (i + by) % size) for i in range(size)])


def from_root(value, axis, root):
    return lax.dynamic_index_in_dim(lax.all_gather(value, axis), root, 0, keepdims=False)


def layer_norm(values, gain_vector):
    average = jnp.mean(values, axis=-1, keepdims=True)
    centred = values - average
    spread = jnp.mean(centred * centred, axis=-1, keepdims=True)
    return centred * lax.rsqrt(spread + epsilon) * gain_vector.astype(jnp.float32)


def attend(normed, w_merged, live_count, head_dim):
    row_count = normed.shape[0]
    merged = jnp.dot(
        normed, w_merged.reshape(w_merged.shape[0], -1), preferred_element_type=jnp.float32
    )
    merged = merged.reshape(row_count, 3, -1, head_dim)
    scores = jnp.einsum(
        "qhd,khd->hqk", merged[:, 0], merged[:, 1], precision=lax.Precision.HIGHEST
    ) * head_dim ** (-0.5)
    visible = jnp.arange(row_count) < live_count
    scores = jnp.where(visible[None, None, :], scores, -1e30)
    weights = jax.nn.softmax(scores, axis=-1)
    mixed = jnp.einsum("hqk,khd->qhd", weights, merged[:, 2], precision=lax.Precision.HIGHEST)
    return mixed.reshape(row_count, -1).astype(jnp.bfloat16)


def local(
    tokens,
    counts,
    assign,
    qkv_weight,
    out_weight,
    up_weight,
    up_bias,
    down_weight,
    attn_gain,
    mlp_gain,
    final_gain,
):
    groups = lax.axis_size("dp")
    sections = lax.axis_size("section")
    tensor_ranks = lax.axis_size("tensor")
    images_dev, block_rows, model_width = tokens.shape
    quarter = model_width // tensor_ranks
    capacity = (images_dev + groups - 1) // groups
    total_images = assign.shape[0]
    batch_images = MICRO
    batch_count = images_dev // batch_images
    my_group = lax.axis_index("dp")
    my_section = lax.axis_index("section")
    tensor_index = lax.axis_index("tensor")
    numbers = jnp.arange(total_images, dtype=jnp.int32)
    matches = (assign[:, None] == numbers[None, :]).astype(jnp.int32)
    slot_of = jnp.sum(matches * numbers[:, None], axis=0)
    target = slot_of // images_dev
    source_group = numbers // images_dev
    earlier = (
        (source_group[:, None] == source_group[None, :])
        & (target[:, None] == target[None, :])
        & (numbers[None, :] < numbers[:, None])
    )
    rank_all = jnp.sum(earlier.astype(jnp.int32), axis=1)
    send_slot = lax.dynamic_slice_in_dim(
        target * capacity + rank_all, my_group * images_dev, images_dev
    )
    buffer_slots = jnp.arange(groups * capacity, dtype=jnp.int32)
    selector = (buffer_slots[:, None] == send_slot[None, :]).astype(jnp.bfloat16)
    outgoing = jnp.einsum(
        "sl,lbd->sbd", selector, tokens, preferred_element_type=jnp.float32
    ).astype(jnp.bfloat16)
    received = cut_exchange(outgoing, "dp", 2, 0, 0)
    my_images = lax.dynamic_slice_in_dim(assign, my_group * images_dev, images_dev)
    chosen = (my_images[:, None] == numbers[None, :]).astype(jnp.int32)
    receive_slot = jnp.sum(chosen * (source_group * capacity + rank_all)[None, :], axis=1)
    live_counts = jnp.sum(chosen * counts[None, :], axis=1)
    picker = (buffer_slots[None, :] == receive_slot[:, None]).astype(jnp.bfloat16)
    arrived = jnp.einsum(
        "js,sbd->jbd", picker, received, preferred_element_type=jnp.float32
    ).astype(jnp.bfloat16)
    arrived_batches = arrived.reshape(batch_count, batch_images, block_rows, model_width)
    live_batches = live_counts.reshape(batch_count, batch_images)
    qkv_full, out_full, up_full, down_full = rows_first(
        (qkv_weight, out_weight, up_weight, down_weight), "dp", (1, 1, 1, 2)
    )
    qkv_full = qkv_full[0]
    out_full = out_full[0]
    up_full = up_full[0]
    down_full = down_full[0]
    bias_row = up_bias[0].astype(jnp.float32)
    gain_attn = attn_gain[0]
    gain_mlp = mlp_gain[0]
    row_numbers = jnp.arange(block_rows)
    flat_rows = batch_images * block_rows

    def advance(step_index, state):
        carried, stored = state
        current = carried
        done_index = step_index - sections
        finishing = (my_section == 0) & (done_index >= 0)
        done_slot = jnp.clip(done_index, 0, batch_count - 1)
        finished_rows = row_numbers[None, :, None] < live_batches[done_slot][:, None, None]
        finished = jnp.where(
            finished_rows, layer_norm(current.astype(jnp.float32), final_gain), 0.0
        ).astype(jnp.bfloat16)
        stored = jnp.where(
            finishing, lax.dynamic_update_index_in_dim(stored, finished, done_slot, 0), stored
        )
        micro_index = step_index - my_section
        active = (micro_index >= 0) & (micro_index < batch_count)
        slot_index = jnp.clip(micro_index, 0, batch_count - 1)
        injected = lax.dynamic_index_in_dim(
            arrived_batches, jnp.clip(step_index, 0, batch_count - 1), 0, keepdims=False
        )
        incoming = jnp.where(my_section == 0, injected, current)
        live_now = live_batches[slot_index]

        def attention_part():
            normed = layer_norm(incoming.astype(jnp.float32), gain_attn).astype(jnp.bfloat16)
            return jax.vmap(
                lambda image_rows, live_count: attend(image_rows, qkv_full, live_count, HEAD_DIM)
            )(normed, live_now)

        def attention_spare():
            return jnp.zeros((batch_images, block_rows, quarter), jnp.bfloat16)

        head_out = lax.cond(active, attention_part, attention_spare)
        joined = lax.all_gather(head_out, "tensor", axis=2, tiled=True)

        def mlp_part():
            middle = incoming.reshape(flat_rows, model_width).astype(jnp.float32) + jnp.dot(
                joined.reshape(flat_rows, model_width), out_full, preferred_element_type=jnp.float32
            )
            normed_mlp = layer_norm(middle, gain_mlp).astype(jnp.bfloat16)
            hidden = jax.nn.gelu(
                jnp.dot(normed_mlp, up_full, preferred_element_type=jnp.float32) + bias_row,
                approximate=False,
            ).astype(jnp.bfloat16)
            return (middle, jnp.dot(hidden, down_full, preferred_element_type=jnp.float32))

        def mlp_spare():
            empty = jnp.zeros((flat_rows, model_width), jnp.float32)
            return (empty, empty)

        middle, partial_value = lax.cond(active, mlp_part, mlp_spare)
        summed = over_pieces(partial_value.astype(jnp.bfloat16), "tensor").astype(jnp.float32)
        updated = (
            (middle + summed).astype(jnp.bfloat16).reshape(batch_images, block_rows, model_width)
        )
        carried = passed_along(updated, "section", 1)
        return (carried, stored)

    initial = (
        jnp.zeros((batch_images, block_rows, model_width), jnp.bfloat16),
        jnp.zeros((batch_count, batch_images, block_rows, model_width), jnp.bfloat16),
    )
    carried, stored = lax.fori_loop(0, batch_count + sections, advance, initial)
    stored = stored.reshape(images_dev, block_rows, model_width)
    my_piece = lax.dynamic_slice_in_dim(stored, tensor_index * quarter, quarter, 2)
    spread = from_root(my_piece, "section", 0)
    section_rows = block_rows // sections
    return lax.dynamic_slice_in_dim(spread, my_section * section_rows, section_rows, 1)


def solution(mesh):
    in_specs = (
        P("dp", None, None),
        P(),
        P(),
        P("section", "dp", None, "tensor"),
        P("section", "dp", None),
        P("section", "dp", "tensor"),
        P("section", "tensor"),
        P("section", "tensor", "dp"),
        P("section", None),
        P("section", None),
        P(),
    )
    out_specs = P("dp", "section", "tensor")
    return jax.shard_map(local, mesh=mesh, in_specs=in_specs, out_specs=out_specs, check_vma=False)
```

profile of v0, /device:TPU:1, one launch (start us, length us, event | category | flops | bytes accessed | tf_op | source)
XLA Modules:
  0.0 434.2 jit_solution(15417628559894977373)
XLA Ops:
  13.5 11.3 %all-to-all-start = ((bf16[32,1,16,1024]{3,2,1,0:T(8,128)(2,1)}), bf16[32,1,16,1024]{3,2,1,0:T(8,128)(2,1)S(1)}, u32[]{:S(2)}, u32[]{:S(2)}) async-start(bf16[32,1,16,1024]{3,2,1,0:T(8,128)(2,1)} %copy.71), calls=%async_computation | async-start | bytes 2097152 | tf_op jit(solution)/shard_map/all_to_all | solution.py:34
  26.4 20.6 %all-to-all-done = bf16[32,1,16,1024]{3,2,1,0:T(8,128)(2,1)S(1)} async-done(((bf16[32,1,16,1024]{3,2,1,0:T(8,128)(2,1)}), bf16[32,1,16,1024]{3,2,1,0:T(8,128)(2,1)S(1)}, u32[]{:S(2)}, u32[]{:S(2)}) %all-to-all-start) | async-done | bytes 1048608 | tf_op jit(solution)/shard_map/all_to_all | solution.py:34
  53.7 20.1 %all-to-all-done.1 = bf16[32,1,16,1024]{3,2,1,0:T(8,128)(2,1)S(1)} async-done(((bf16[32,1,16,1024]{3,2,1,0:T(8,128)(2,1)}), bf16[32,1,16,1024]{3,2,1,0:T(8,128)(2,1)S(1)}, u32[]{:S(2)}, u32[]{:S(2)}) %all-to-all-start.1) | async-done | bytes 1048608 | tf_op jit(solution)/shard_map/all_to_all | solution.py:34
  77.7 87.1 %all-gather.8.cloned.1.call-done = bf16[1024,6656]{1,0:T(8,128)(2,1)} async-done(((bf16[32,6656]{1,0:T(8,128)(2,1)}), bf16[1024,6656]{1,0:T(8,128)(2,1)}) %all-gather.8.cloned.1.call-update) | async-done | bytes 13631504 | tf_op jit(solution)/shard_map/all_gather | solution.py:42
  170.8 6.4 %copy.77 = bf16[2048,1024]{1,0:T(8,128)(2,1)} copy(bf16[2048,1024]{0,1:T(8,128)(2,1)} %get-tuple-element.580) | data formatting | bytes 8388608
  185.3 228.6 %while.18 = (s32[]{:T(128)}, bf16[4,32,1024]{2,1,0:T(8,128)(2,1)S(1)}, bf16[4,4,32,1024]{3,2,1,0:T(8,128)(2,1)}, s32[]{:T(128)}, pred[]{:T(512)}, /*index=5*/bf1...) while((s32[]{:T(128)}, ...), condition=%wide.region_18.19_spmd.clone, body=%wide.region_4.18_spmd.clone.sunk | while | flops 1818134144 | bytes 30876236 | solution.py:217
  198.9 25.8 %collective-permute-start = (bf16[4,32,1024]{2,1,0:T(8,128)(2,1)S(1)}, bf16[4,32,1024]{2,1,0:T(8,128)(2,1)S(1)}, u32[]{:S(2)}, u32[]{:S(2)}) collective-permute-start(bf16[4,32,1024]{2,1,0:T(8,128)(2,1)S(1)} %bitcast.86), channel_id=1, source_target_pairs={{0,2},{2,0},{1,3},{3,1},{4,6},{6,4},{5,7},{7,5},{8,10},{10,8},{9,1... | collective-permute-start | bytes 786440 | tf_op jit(solution)/shard_map/while/body/eval_jaxpr/ppermute | solution.py:58
  228.1 11.5 %conditional.6 = (bf16[4,32,512]{2,1,0:T(8,128)(2,1)S(1)}) conditional(s32[]{:T(128)} %convert_element_type.214, () %tuple.78, (bf16[4,32,1024]{2,1,0:T(8,128)(2,1)S(1)}, bf16[1024]{0:T(1024)(128)(2,1)S(1)}, bf16[1024,1536]{1,0:T(8,128)(2,1)}, s32[]{:T(128)}, s32[4,4]{1,0:T(4,128)S(1)}) %tuple.79), branch_computations={%region_5.5_spmd, %region_6.10_spmd} | conditional | flops 454720768 | bytes 9734996 | solution.py:187
  245.3 11.4 %conditional.7 = (f32[128,1024]{1,0:T(8,128)}, f32[128,1024]{1,0:T(8,128)S(1)}) conditional(s32[]{:T(128)} %convert_element_type.214, () %tuple.77, (bf16[4,32,1024]{2,1,0:T(8,128)(2,1)S(1)}, bf16[4,32,1024]{2,1,0:T(8,128)(2,1)S(1)}, bf16[1024,1024]{1,0:T(8,128)(2,1)}, bf16[1024]{0:T(1024)(128)(2,1)S(1)}, bf16[1024,2048]{1,0:T(8,128)(2,1)}, ...), branch_computations={%region_11.11_spmd, %region_12.14_spmd} | conditional | flops 1360790656 | bytes 13130256 | solution.py:205
  249.4 7.3 %fusion.29 = f32[128,1024]{1,0:T(8,128)S(1)} fusion(bf16[2048,1024]{1,0:T(8,128)(2,1)} %get-tuple-element.410, bf16[1024,2048]{1,0:T(8,128)(2,1)} %get-tuple-element.408, f32[2048]{0:T(1024)S(1)} %get-tuple-element.409, f32[128,1024]{1,0:T(8,128)} %get-tuple-element.685, f32[1024]{0:T(1024)S(1)} %convert_element_type.116, f32[128]{0:T(128)S(1)} %add_rsqrt_fusion.1, ...), kind=kOutput, calls=%fused_computation.50 | convolution fusion | flops 1091567616 | bytes 9450496 | tf_op jit(solution)/shard_map/while/body/eval_jaxpr/cond/branch_1_fun/dot_general | solution.py:199
  256.8 7.6 %all-gather.4 = bf16[256,1024]{1,0:T(8,128)(2,1)S(1)} all-gather(bf16[128,1024]{1,0:T(8,128)(2,1)S(1)} %convert_element_type.215), channel_id=2, replica_groups=mesh['dp'=32,'section'=2,'tensor'=2] {'tensor'}, dimensions={0}, use_global_device_ids=true | all-gather | bytes 786432 | tf_op jit(solution)/shard_map/while/body/eval_jaxpr/all_gather | solution.py:53
  270.9 11.5 %conditional.6 = (bf16[4,32,512]{2,1,0:T(8,128)(2,1)S(1)}) conditional(s32[]{:T(128)} %convert_element_type.214, () %tuple.78, (bf16[4,32,1024]{2,1,0:T(8,128)(2,1)S(1)}, bf16[1024]{0:T(1024)(128)(2,1)S(1)}, bf16[1024,1536]{1,0:T(8,128)(2,1)}, s32[]{:T(128)}, s32[4,4]{1,0:T(4,128)S(1)}) %tuple.79), branch_computations={%region_5.5_spmd, %region_6.10_spmd} | conditional | flops 454720768 | bytes 9734996 | solution.py:187
  288.1 11.4 %conditional.7 = (f32[128,1024]{1,0:T(8,128)}, f32[128,1024]{1,0:T(8,128)S(1)}) conditional(s32[]{:T(128)} %convert_element_type.214, () %tuple.77, (bf16[4,32,1024]{2,1,0:T(8,128)(2,1)S(1)}, bf16[4,32,1024]{2,1,0:T(8,128)(2,1)S(1)}, bf16[1024,1024]{1,0:T(8,128)(2,1)}, bf16[1024]{0:T(1024)(128)(2,1)S(1)}, bf16[1024,2048]{1,0:T(8,128)(2,1)}, ...), branch_computations={%region_11.11_spmd, %region_12.14_spmd} | conditional | flops 1360790656 | bytes 13130256 | solution.py:205
  292.2 7.3 %fusion.29 = f32[128,1024]{1,0:T(8,128)S(1)} fusion(bf16[2048,1024]{1,0:T(8,128)(2,1)} %get-tuple-element.410, bf16[1024,2048]{1,0:T(8,128)(2,1)} %get-tuple-element.408, f32[2048]{0:T(1024)S(1)} %get-tuple-element.409, f32[128,1024]{1,0:T(8,128)} %get-tuple-element.685, f32[1024]{0:T(1024)S(1)} %convert_element_type.116, f32[128]{0:T(128)S(1)} %add_rsqrt_fusion.1, ...), kind=kOutput, calls=%fused_computation.50 | convolution fusion | flops 1091567616 | bytes 9450496 | tf_op jit(solution)/shard_map/while/body/eval_jaxpr/cond/branch_1_fun/dot_general | solution.py:199
  299.6 7.6 %all-gather.4 = bf16[256,1024]{1,0:T(8,128)(2,1)S(1)} all-gather(bf16[128,1024]{1,0:T(8,128)(2,1)S(1)} %convert_element_type.215), channel_id=2, replica_groups=mesh['dp'=32,'section'=2,'tensor'=2] {'tensor'}, dimensions={0}, use_global_device_ids=true | all-gather | bytes 786432 | tf_op jit(solution)/shard_map/while/body/eval_jaxpr/all_gather | solution.py:53
  313.7 11.5 %conditional.6 = (bf16[4,32,512]{2,1,0:T(8,128)(2,1)S(1)}) conditional(s32[]{:T(128)} %convert_element_type.214, () %tuple.78, (bf16[4,32,1024]{2,1,0:T(8,128)(2,1)S(1)}, bf16[1024]{0:T(1024)(128)(2,1)S(1)}, bf16[1024,1536]{1,0:T(8,128)(2,1)}, s32[]{:T(128)}, s32[4,4]{1,0:T(4,128)S(1)}) %tuple.79), branch_computations={%region_5.5_spmd, %region_6.10_spmd} | conditional | flops 454720768 | bytes 9734996 | solution.py:187
  330.9 11.4 %conditional.7 = (f32[128,1024]{1,0:T(8,128)}, f32[128,1024]{1,0:T(8,128)S(1)}) conditional(s32[]{:T(128)} %convert_element_type.214, () %tuple.77, (bf16[4,32,1024]{2,1,0:T(8,128)(2,1)S(1)}, bf16[4,32,1024]{2,1,0:T(8,128)(2,1)S(1)}, bf16[1024,1024]{1,0:T(8,128)(2,1)}, bf16[1024]{0:T(1024)(128)(2,1)S(1)}, bf16[1024,2048]{1,0:T(8,128)(2,1)}, ...), branch_computations={%region_11.11_spmd, %region_12.14_spmd} | conditional | flops 1360790656 | bytes 13130256 | solution.py:205
  335.0 7.3 %fusion.29 = f32[128,1024]{1,0:T(8,128)S(1)} fusion(bf16[2048,1024]{1,0:T(8,128)(2,1)} %get-tuple-element.410, bf16[1024,2048]{1,0:T(8,128)(2,1)} %get-tuple-element.408, f32[2048]{0:T(1024)S(1)} %get-tuple-element.409, f32[128,1024]{1,0:T(8,128)} %get-tuple-element.685, f32[1024]{0:T(1024)S(1)} %convert_element_type.116, f32[128]{0:T(128)S(1)} %add_rsqrt_fusion.1, ...), kind=kOutput, calls=%fused_computation.50 | convolution fusion | flops 1091567616 | bytes 9450496 | tf_op jit(solution)/shard_map/while/body/eval_jaxpr/cond/branch_1_fun/dot_general | solution.py:199
  342.4 7.6 %all-gather.4 = bf16[256,1024]{1,0:T(8,128)(2,1)S(1)} all-gather(bf16[128,1024]{1,0:T(8,128)(2,1)S(1)} %convert_element_type.215), channel_id=2, replica_groups=mesh['dp'=32,'section'=2,'tensor'=2] {'tensor'}, dimensions={0}, use_global_device_ids=true | all-gather | bytes 786432 | tf_op jit(solution)/shard_map/while/body/eval_jaxpr/all_gather | solution.py:53
  356.5 11.5 %conditional.6 = (bf16[4,32,512]{2,1,0:T(8,128)(2,1)S(1)}) conditional(s32[]{:T(128)} %convert_element_type.214, () %tuple.78, (bf16[4,32,1024]{2,1,0:T(8,128)(2,1)S(1)}, bf16[1024]{0:T(1024)(128)(2,1)S(1)}, bf16[1024,1536]{1,0:T(8,128)(2,1)}, s32[]{:T(128)}, s32[4,4]{1,0:T(4,128)S(1)}) %tuple.79), branch_computations={%region_5.5_spmd, %region_6.10_spmd} | conditional | flops 454720768 | bytes 9734996 | solution.py:187
  372.5 11.4 %conditional.7 = (f32[128,1024]{1,0:T(8,128)}, f32[128,1024]{1,0:T(8,128)S(1)}) conditional(s32[]{:T(128)} %convert_element_type.214, () %tuple.77, (bf16[4,32,1024]{2,1,0:T(8,128)(2,1)S(1)}, bf16[4,32,1024]{2,1,0:T(8,128)(2,1)S(1)}, bf16[1024,1024]{1,0:T(8,128)(2,1)}, bf16[1024]{0:T(1024)(128)(2,1)S(1)}, bf16[1024,2048]{1,0:T(8,128)(2,1)}, ...), branch_computations={%region_11.11_spmd, %region_12.14_spmd} | conditional | flops 1360790656 | bytes 13130256 | solution.py:205
  376.6 7.3 %fusion.29 = f32[128,1024]{1,0:T(8,128)S(1)} fusion(bf16[2048,1024]{1,0:T(8,128)(2,1)} %get-tuple-element.410, bf16[1024,2048]{1,0:T(8,128)(2,1)} %get-tuple-element.408, f32[2048]{0:T(1024)S(1)} %get-tuple-element.409, f32[128,1024]{1,0:T(8,128)} %get-tuple-element.685, f32[1024]{0:T(1024)S(1)} %convert_element_type.116, f32[128]{0:T(128)S(1)} %add_rsqrt_fusion.1, ...), kind=kOutput, calls=%fused_computation.50 | convolution fusion | flops 1091567616 | bytes 9450496 | tf_op jit(solution)/shard_map/while/body/eval_jaxpr/cond/branch_1_fun/dot_general | solution.py:199
  400.8 7.2 %all-gather.4 = bf16[256,1024]{1,0:T(8,128)(2,1)S(1)} all-gather(bf16[128,1024]{1,0:T(8,128)(2,1)S(1)} %convert_element_type.215), channel_id=2, replica_groups=mesh['dp'=32,'section'=2,'tensor'=2] {'tensor'}, dimensions={0}, use_global_device_ids=true | all-gather | bytes 786432 | tf_op jit(solution)/shard_map/while/body/eval_jaxpr/all_gather | solution.py:53
  415.9 9.7 %all-gather.10.cloned.1.call-done = bf16[32,32,512]{2,1,0:T(8,128)(2,1)} async-done(((bf16[16,32,512]{2,1,0:T(8,128)(2,1)}), bf16[32,32,512]{2,1,0:T(8,128)(2,1)}) %all-gather.10.cloned.1.call-update) | async-done | bytes 1048592 | tf_op jit(solution)/shard_map/all_gather | solution.py:62
  (234 shorter events, 181.3 us)
Async XLA Ops:
  6.5 4.2 copy-start
  6.5 158.2 %all-gather.8.cloned.1.call-start = ((), (), s32[]{:S(2)}) async-start(), calls=%async_computation.2 | async-start | bytes 14057472 | tf_op jit(solution)/shard_map/all_gather | solution.py:42
  11.9 39.9 %copy-start.5 = (s32[512]{0:T(512)S(1)}, s32[512]{0:T(512)}, u32[]{:S(2)}) copy-start(s32[512]{0:T(512)} %param.18) | copy-start | bytes 6148
  11.9 40.2 %copy-start.2 = (bf16[1,2048]{1,0:T(2,128)(2,1)S(1)}, bf16[1,2048]{1,0:T(2,128)(2,1)}, u32[]{:S(2)}) copy-start(bf16[1,2048]{1,0:T(2,128)(2,1)} %param.23) | copy-start | bytes 12292
  11.9 40.2 %copy-start.3 = (bf16[1,1024]{1,0:T(2,128)(2,1)S(1)}, bf16[1,1024]{1,0:T(2,128)(2,1)}, u32[]{:S(2)}) copy-start(bf16[1,1024]{1,0:T(2,128)(2,1)} %param.25) | copy-start | bytes 6148
  12.0 40.2 %copy-start.4 = (bf16[1,1024]{1,0:T(2,128)(2,1)S(1)}, bf16[1,1024]{1,0:T(2,128)(2,1)}, u32[]{:S(2)}) copy-start(bf16[1,1024]{1,0:T(2,128)(2,1)} %param.26) | copy-start | bytes 6148
  13.5 33.5 %all-to-all-start = ((bf16[32,1,16,1024]{3,2,1,0:T(8,128)(2,1)}), bf16[32,1,16,1024]{3,2,1,0:T(8,128)(2,1)S(1)}, u32[]{:S(2)}, u32[]{:S(2)}) async-start(bf16[32,1,16,1024]{3,2,1,0:T(8,128)(2,1)} %copy.71), calls=%async_computation | async-start | bytes 2097152 | tf_op jit(solution)/shard_map/all_to_all | solution.py:34
  47.0 26.8 %all-to-all-start.1 = ((bf16[32,1,16,1024]{3,2,1,0:T(8,128)(2,1)}), bf16[32,1,16,1024]{3,2,1,0:T(8,128)(2,1)S(1)}, u32[]{:S(2)}, u32[]{:S(2)}) async-start(bf16[32,1,16,1024]{3,2,1,0:T(8,128)(2,1)} %copy.72), calls=%async_computation.1 | async-start | bytes 2097152 | tf_op jit(solution)/shard_map/all_to_all | solution.py:34
  51.0 374.6 %all-gather.10.cloned.1.call-start = ((), (), s32[]{:S(2)}) async-start(), calls=%async_computation.3 | async-start | bytes 1572864 | tf_op jit(solution)/shard_map/all_gather | solution.py:62
  181.0 4.3 copy-start.1
  198.9 28.2 %collective-permute-start = (bf16[4,32,1024]{2,1,0:T(8,128)(2,1)S(1)}, bf16[4,32,1024]{2,1,0:T(8,128)(2,1)S(1)}, u32[]{:S(2)}, u32[]{:S(2)}) collective-permute-start(bf16[4,32,1024]{2,1,0:T(8,128)(2,1)S(1)} %bitcast.86), channel_id=1, source_target_pairs={{0,2},{2,0},{1,3},{3,1},{4,6},{6,4},{5,7},{7,5},{8,10},{10,8},{9,1... | collective-permute-start | bytes 786440 | tf_op jit(solution)/shard_map/while/body/eval_jaxpr/ppermute | solution.py:58
  265.7 4.2 collective-permute-start
  308.5 4.2 collective-permute-start
  351.3 4.2 collective-permute-start
  391.1 2.5 collective-permute-start
  409.2 4.7 %collective-permute-start = (bf16[4,32,1024]{2,1,0:T(8,128)(2,1)S(1)}, bf16[4,32,1024]{2,1,0:T(8,128)(2,1)S(1)}, u32[]{:S(2)}, u32[]{:S(2)}) collective-permute-start(bf16[4,32,1024]{2,1,0:T(8,128)(2,1)S(1)} %bitcast.86), channel_id=1, source_target_pairs={{0,2},{2,0},{1,3},{3,1},{4,6},{6,4},{5,7},{7,5},{8,10},{10,8},{9,1... | collective-permute-start | bytes 786440 | tf_op jit(solution)/shard_map/while/body/eval_jaxpr/ppermute | solution.py:58
Sparse Core Ops, SparseCore 0:
  10.5 154.2 all-gather.7
  416.0 9.5 all-gather.9
where the time goes:
time: 437 us; the launch traced here: 434 us
  waiting for transfers between devices  137 us (31%)
  matrix products  74.6 us (17%)
  blocking collectives  73.2 us (17%)
  starting transfers between devices  49 us (11%)
  local copies, waits for them, and re-layouts  47.6 us (11%)
  other arithmetic  37.8 us (9%)
  between operations  13.6 us (3%)
    all_gather x1, waiting for transfers between devices, rows_first(): out = lax.all_gather(both, axis, axis=0, tiled=True)  87.1 us
    all_gather x6, blocking collectives, over_pieces(): return lax.all_gather(value, axis).astype(jnp.float32).sum(0)  41.9 us
    all_to_all x2, waiting for transfers between devices, cut_exchange(): lax.all_to_all(section, axis, split_axis=0, concat_axis=0, tiled=True)  40.7 us
    ppermute x6, starting transfers between devices, passed_along(): lax.ppermute(value, axis, [(i, (i + by) % size) for i in range(size)])  33.6 us
    all_gather x6, blocking collectives, advance(): joined = lax.all_gather(head_out, 'tensor', axis=2, tiled=True)  31.3 us
    dot_general x4, matrix products, mlp_part(): jnp.dot(hidden, down_full, preferred_element_type=jnp.float32)  29.2 us
    all_to_all x2, starting transfers between devices, cut_exchange(): lax.all_to_all(section, axis, split_axis=0, concat_axis=0, tiled=True)  15.3 us
    dot_general x4, matrix products, attend(): jnp.dot(normed, w_merged.reshape(w_merged.shape[0], -1), preferred_elemen...  13.8 us
  transfers between devices with their start and end apart: 10, of which 4 were waited for; matrix products, arithmetic and copies ran while one was open for 6% of the time, Pallas kernels for 0%

commit v1 on v0

--- a/solution.py
+++ b/solution.py
@@ -185,7 +185,8 @@
             return jnp.zeros((batch_images, block_rows, quarter), jnp.bfloat16)
 
         head_out = lax.cond(active, attention_part, attention_spare)
-        joined = lax.all_gather(head_out, "tensor", axis=2, tiled=True)
+        blocks = lax.all_gather(head_out, "tensor")
+        joined = jnp.concatenate(blocks, axis=2)
 
         def mlp_part():
             middle = incoming.reshape(flat_rows, model_width).astype(jnp.float32) + jnp.dot(

time: 437 us -> 438 us (level)
  no operation moved by 1% of the time
where the time goes in v1:
time: 438 us; the launch traced here: 436 us
  waiting for transfers between devices  137 us (31%)
  matrix products  74.7 us (17%)
  blocking collectives  73.2 us (17%)
  starting transfers between devices  49.3 us (11%)
  local copies, waits for them, and re-layouts  48.9 us (11%)
  other arithmetic  37.8 us (9%)
  between operations  13.6 us (3%)
    all_gather x1, waiting for transfers between devices, rows_first(): out = lax.all_gather(both, axis, axis=0, tiled=True)  87.1 us
    all_gather x6, blocking collectives, over_pieces(): return lax.all_gather(value, axis).astype(jnp.float32).sum(0)  41.9 us
    all_to_all x2, waiting for transfers between devices, cut_exchange(): lax.all_to_all(section, axis, split_axis=0, concat_axis=0, tiled=True)  40.7 us
    ppermute x6, starting transfers between devices, passed_along(): lax.ppermute(value, axis, [(i, (i + by) % size) for i in range(size)])  33.9 us
    all_gather x6, blocking collectives, advance(): blocks = lax.all_gather(head_out, 'tensor')  31.3 us
    dot_general x4, matrix products, mlp_part(): jnp.dot(hidden, down_full, preferred_element_type=jnp.float32)  29.2 us
    all_to_all x2, starting transfers between devices, cut_exchange(): lax.all_to_all(section, axis, split_axis=0, concat_axis=0, tiled=True)  15.3 us
    dot_general x4, matrix products, attend(): jnp.dot(normed, w_merged.reshape(w_merged.shape[0], -1), preferred_elemen...  13.8 us
  transfers between devices with their start and end apart: 10, of which 4 were waited for; matrix products, arithmetic and copies ran while one was open for 6% of the time, Pallas kernels for 0%

profile of v1, /device:TPU:1, one launch (start us, length us, event | category | flops | bytes accessed | tf_op | source)
XLA Modules:
  0.0 435.8 jit_solution(5650916842259438520)
XLA Ops:
  13.5 11.3 %all-to-all-start = ((bf16[32,1,16,1024]{3,2,1,0:T(8,128)(2,1)}), bf16[32,1,16,1024]{3,2,1,0:T(8,128)(2,1)S(1)}, u32[]{:S(2)}, u32[]{:S(2)}) async-start(bf16[32,1,16,1024]{3,2,1,0:T(8,128)(2,1)} %copy.75), calls=%async_computation | async-start | bytes 2097152 | tf_op jit(solution)/shard_map/all_to_all | solution.py:34
  26.4 20.6 %all-to-all-done = bf16[32,1,16,1024]{3,2,1,0:T(8,128)(2,1)S(1)} async-done(((bf16[32,1,16,1024]{3,2,1,0:T(8,128)(2,1)}), bf16[32,1,16,1024]{3,2,1,0:T(8,128)(2,1)S(1)}, u32[]{:S(2)}, u32[]{:S(2)}) %all-to-all-start) | async-done | bytes 1048608 | tf_op jit(solution)/shard_map/all_to_all | solution.py:34
  53.7 20.1 %all-to-all-done.1 = bf16[32,1,16,1024]{3,2,1,0:T(8,128)(2,1)S(1)} async-done(((bf16[32,1,16,1024]{3,2,1,0:T(8,128)(2,1)}), bf16[32,1,16,1024]{3,2,1,0:T(8,128)(2,1)S(1)}, u32[]{:S(2)}, u32[]{:S(2)}) %all-to-all-start.1) | async-done | bytes 1048608 | tf_op jit(solution)/shard_map/all_to_all | solution.py:34
  77.7 87.1 %all-gather.12.cloned.1.call-done = bf16[1024,6656]{1,0:T(8,128)(2,1)} async-done(((bf16[32,6656]{1,0:T(8,128)(2,1)}), bf16[1024,6656]{1,0:T(8,128)(2,1)}) %all-gather.12.cloned.1.call-update) | async-done | bytes 13631504 | tf_op jit(solution)/shard_map/all_gather | solution.py:42
  170.8 6.4 %copy.81 = bf16[2048,1024]{1,0:T(8,128)(2,1)} copy(bf16[2048,1024]{0,1:T(8,128)(2,1)} %get-tuple-element.608) | data formatting | bytes 8388608
  185.3 230.2 %while.18 = (s32[]{:T(128)}, bf16[4,32,1024]{2,1,0:T(8,128)(2,1)S(1)}, bf16[4,4,32,1024]{3,2,1,0:T(8,128)(2,1)}, s32[]{:T(128)}, pred[]{:T(512)}, /*index=5*/bf1...) while((s32[]{:T(128)}, ...), condition=%wide.region_18.19_spmd.clone, body=%wide.region_4.18_spmd.clone.sunk | while | flops 1818134144 | bytes 31924812 | solution.py:218
  198.9 26.1 %collective-permute-start = (bf16[4,32,1024]{2,1,0:T(8,128)(2,1)S(1)}, bf16[4,32,1024]{2,1,0:T(8,128)(2,1)S(1)}, u32[]{:S(2)}, u32[]{:S(2)}) collective-permute-start(bf16[4,32,1024]{2,1,0:T(8,128)(2,1)S(1)} %bitcast.95), channel_id=1, source_target_pairs={{0,2},{2,0},{1,3},{3,1},{4,6},{6,4},{5,7},{7,5},{8,10},{10,8},{9,1... | collective-permute-start | bytes 786440 | tf_op jit(solution)/shard_map/while/body/eval_jaxpr/ppermute | solution.py:58
  228.4 11.5 %conditional.6 = (bf16[4,32,512]{2,1,0:T(8,128)(2,1)S(1)}) conditional(s32[]{:T(128)} %convert_element_type.214, () %tuple.82, (bf16[4,32,1024]{2,1,0:T(8,128)(2,1)S(1)}, bf16[1024]{0:T(1024)(128)(2,1)S(1)}, bf16[1024,1536]{1,0:T(8,128)(2,1)}, s32[]{:T(128)}, s32[4,4]{1,0:T(4,128)S(1)}) %tuple.83), branch_computations={%region_5.5_spmd, %region_6.10_spmd} | conditional | flops 454720768 | bytes 9734996 | solution.py:187
  245.6 11.7 %conditional.7 = (f32[128,1024]{1,0:T(8,128)}, f32[128,1024]{1,0:T(8,128)S(1)}) conditional(s32[]{:T(128)} %convert_element_type.214, () %tuple.81, (bf16[4,32,1024]{2,1,0:T(8,128)(2,1)S(1)}, bf16[4,32,2,512]{3,1,0,2:T(8,128)(2,1)S(1)}, bf16[1024,1024]{1,0:T(8,128)(2,1)}, bf16[1024]{0:T(1024)(128)(2,1)S(1)}, bf16[1024,2048]{1,0:T(8,128)(2,1)}, ...), branch_computations={%region_11.11_spmd, %region_12.14_spmd} | conditional | flops 1360790656 | bytes 14178832 | solution.py:206
  250.1 7.3 %fusion.29 = f32[128,1024]{1,0:T(8,128)S(1)} fusion(bf16[2048,1024]{1,0:T(8,128)(2,1)} %get-tuple-element.410, bf16[1024,2048]{1,0:T(8,128)(2,1)} %get-tuple-element.408, f32[2048]{0:T(1024)S(1)} %get-tuple-element.409, f32[128,1024]{1,0:T(8,128)} %get-tuple-element.713, f32[1024]{0:T(1024)S(1)} %convert_element_type.116, f32[128]{0:T(128)S(1)} %add_rsqrt_fusion.1, ...), kind=kOutput, calls=%fused_computation.50 | convolution fusion | flops 1091567616 | bytes 9450496 | tf_op jit(solution)/shard_map/while/body/eval_jaxpr/cond/branch_1_fun/dot_general | solution.py:200
  257.4 7.6 %all-gather.8 = bf16[256,1024]{1,0:T(8,128)(2,1)S(1)} all-gather(bf16[128,1024]{1,0:T(8,128)(2,1)S(1)} %convert_element_type.215), channel_id=3, replica_groups=mesh['dp'=32,'section'=2,'tensor'=2] {'tensor'}, dimensions={0}, use_global_device_ids=true | all-gather | bytes 786432 | tf_op jit(solution)/shard_map/while/body/eval_jaxpr/all_gather | solution.py:53
  271.5 11.5 %conditional.6 = (bf16[4,32,512]{2,1,0:T(8,128)(2,1)S(1)}) conditional(s32[]{:T(128)} %convert_element_type.214, () %tuple.82, (bf16[4,32,1024]{2,1,0:T(8,128)(2,1)S(1)}, bf16[1024]{0:T(1024)(128)(2,1)S(1)}, bf16[1024,1536]{1,0:T(8,128)(2,1)}, s32[]{:T(128)}, s32[4,4]{1,0:T(4,128)S(1)}) %tuple.83), branch_computations={%region_5.5_spmd, %region_6.10_spmd} | conditional | flops 454720768 | bytes 9734996 | solution.py:187
  288.7 11.8 %conditional.7 = (f32[128,1024]{1,0:T(8,128)}, f32[128,1024]{1,0:T(8,128)S(1)}) conditional(s32[]{:T(128)} %convert_element_type.214, () %tuple.81, (bf16[4,32,1024]{2,1,0:T(8,128)(2,1)S(1)}, bf16[4,32,2,512]{3,1,0,2:T(8,128)(2,1)S(1)}, bf16[1024,1024]{1,0:T(8,128)(2,1)}, bf16[1024]{0:T(1024)(128)(2,1)S(1)}, bf16[1024,2048]{1,0:T(8,128)(2,1)}, ...), branch_computations={%region_11.11_spmd, %region_12.14_spmd} | conditional | flops 1360790656 | bytes 14178832 | solution.py:206
  293.2 7.3 %fusion.29 = f32[128,1024]{1,0:T(8,128)S(1)} fusion(bf16[2048,1024]{1,0:T(8,128)(2,1)} %get-tuple-element.410, bf16[1024,2048]{1,0:T(8,128)(2,1)} %get-tuple-element.408, f32[2048]{0:T(1024)S(1)} %get-tuple-element.409, f32[128,1024]{1,0:T(8,128)} %get-tuple-element.713, f32[1024]{0:T(1024)S(1)} %convert_element_type.116, f32[128]{0:T(128)S(1)} %add_rsqrt_fusion.1, ...), kind=kOutput, calls=%fused_computation.50 | convolution fusion | flops 1091567616 | bytes 9450496 | tf_op jit(solution)/shard_map/while/body/eval_jaxpr/cond/branch_1_fun/dot_general | solution.py:200
  300.5 7.6 %all-gather.8 = bf16[256,1024]{1,0:T(8,128)(2,1)S(1)} all-gather(bf16[128,1024]{1,0:T(8,128)(2,1)S(1)} %convert_element_type.215), channel_id=3, replica_groups=mesh['dp'=32,'section'=2,'tensor'=2] {'tensor'}, dimensions={0}, use_global_device_ids=true | all-gather | bytes 786432 | tf_op jit(solution)/shard_map/while/body/eval_jaxpr/all_gather | solution.py:53
  314.6 11.5 %conditional.6 = (bf16[4,32,512]{2,1,0:T(8,128)(2,1)S(1)}) conditional(s32[]{:T(128)} %convert_element_type.214, () %tuple.82, (bf16[4,32,1024]{2,1,0:T(8,128)(2,1)S(1)}, bf16[1024]{0:T(1024)(128)(2,1)S(1)}, bf16[1024,1536]{1,0:T(8,128)(2,1)}, s32[]{:T(128)}, s32[4,4]{1,0:T(4,128)S(1)}) %tuple.83), branch_computations={%region_5.5_spmd, %region_6.10_spmd} | conditional | flops 454720768 | bytes 9734996 | solution.py:187
  331.9 11.7 %conditional.7 = (f32[128,1024]{1,0:T(8,128)}, f32[128,1024]{1,0:T(8,128)S(1)}) conditional(s32[]{:T(128)} %convert_element_type.214, () %tuple.81, (bf16[4,32,1024]{2,1,0:T(8,128)(2,1)S(1)}, bf16[4,32,2,512]{3,1,0,2:T(8,128)(2,1)S(1)}, bf16[1024,1024]{1,0:T(8,128)(2,1)}, bf16[1024]{0:T(1024)(128)(2,1)S(1)}, bf16[1024,2048]{1,0:T(8,128)(2,1)}, ...), branch_computations={%region_11.11_spmd, %region_12.14_spmd} | conditional | flops 1360790656 | bytes 14178832 | solution.py:206
  336.3 7.3 %fusion.29 = f32[128,1024]{1,0:T(8,128)S(1)} fusion(bf16[2048,1024]{1,0:T(8,128)(2,1)} %get-tuple-element.410, bf16[1024,2048]{1,0:T(8,128)(2,1)} %get-tuple-element.408, f32[2048]{0:T(1024)S(1)} %get-tuple-element.409, f32[128,1024]{1,0:T(8,128)} %get-tuple-element.713, f32[1024]{0:T(1024)S(1)} %convert_element_type.116, f32[128]{0:T(128)S(1)} %add_rsqrt_fusion.1, ...), kind=kOutput, calls=%fused_computation.50 | convolution fusion | flops 1091567616 | bytes 9450496 | tf_op jit(solution)/shard_map/while/body/eval_jaxpr/cond/branch_1_fun/dot_general | solution.py:200
  343.7 7.6 %all-gather.8 = bf16[256,1024]{1,0:T(8,128)(2,1)S(1)} all-gather(bf16[128,1024]{1,0:T(8,128)(2,1)S(1)} %convert_element_type.215), channel_id=3, replica_groups=mesh['dp'=32,'section'=2,'tensor'=2] {'tensor'}, dimensions={0}, use_global_device_ids=true | all-gather | bytes 786432 | tf_op jit(solution)/shard_map/while/body/eval_jaxpr/all_gather | solution.py:53
  357.8 11.5 %conditional.6 = (bf16[4,32,512]{2,1,0:T(8,128)(2,1)S(1)}) conditional(s32[]{:T(128)} %convert_element_type.214, () %tuple.82, (bf16[4,32,1024]{2,1,0:T(8,128)(2,1)S(1)}, bf16[1024]{0:T(1024)(128)(2,1)S(1)}, bf16[1024,1536]{1,0:T(8,128)(2,1)}, s32[]{:T(128)}, s32[4,4]{1,0:T(4,128)S(1)}) %tuple.83), branch_computations={%region_5.5_spmd, %region_6.10_spmd} | conditional | flops 454720768 | bytes 9734996 | solution.py:187
  373.8 11.7 %conditional.7 = (f32[128,1024]{1,0:T(8,128)}, f32[128,1024]{1,0:T(8,128)S(1)}) conditional(s32[]{:T(128)} %convert_element_type.214, () %tuple.81, (bf16[4,32,1024]{2,1,0:T(8,128)(2,1)S(1)}, bf16[4,32,2,512]{3,1,0,2:T(8,128)(2,1)S(1)}, bf16[1024,1024]{1,0:T(8,128)(2,1)}, bf16[1024]{0:T(1024)(128)(2,1)S(1)}, bf16[1024,2048]{1,0:T(8,128)(2,1)}, ...), branch_computations={%region_11.11_spmd, %region_12.14_spmd} | conditional | flops 1360790656 | bytes 14178832 | solution.py:206
  378.2 7.3 %fusion.29 = f32[128,1024]{1,0:T(8,128)S(1)} fusion(bf16[2048,1024]{1,0:T(8,128)(2,1)} %get-tuple-element.410, bf16[1024,2048]{1,0:T(8,128)(2,1)} %get-tuple-element.408, f32[2048]{0:T(1024)S(1)} %get-tuple-element.409, f32[128,1024]{1,0:T(8,128)} %get-tuple-element.713, f32[1024]{0:T(1024)S(1)} %convert_element_type.116, f32[128]{0:T(128)S(1)} %add_rsqrt_fusion.1, ...), kind=kOutput, calls=%fused_computation.50 | convolution fusion | flops 1091567616 | bytes 9450496 | tf_op jit(solution)/shard_map/while/body/eval_jaxpr/cond/branch_1_fun/dot_general | solution.py:200
  402.4 7.2 %all-gather.8 = bf16[256,1024]{1,0:T(8,128)(2,1)S(1)} all-gather(bf16[128,1024]{1,0:T(8,128)(2,1)S(1)} %convert_element_type.215), channel_id=3, replica_groups=mesh['dp'=32,'section'=2,'tensor'=2] {'tensor'}, dimensions={0}, use_global_device_ids=true | all-gather | bytes 786432 | tf_op jit(solution)/shard_map/while/body/eval_jaxpr/all_gather | solution.py:53
  417.5 9.7 %all-gather.14.cloned.1.call-done = bf16[32,32,512]{2,1,0:T(8,128)(2,1)} async-done(((bf16[16,32,512]{2,1,0:T(8,128)(2,1)}), bf16[32,32,512]{2,1,0:T(8,128)(2,1)}) %all-gather.14.cloned.1.call-update) | async-done | bytes 1048592 | tf_op jit(solution)/shard_map/all_gather | solution.py:62
  (242 shorter events, 182.5 us)
Async XLA Ops:
  6.5 4.2 copy-start
  6.5 158.2 %all-gather.12.cloned.1.call-start = ((), (), s32[]{:S(2)}) async-start(), calls=%async_computation.2 | async-start | bytes 14057472 | tf_op jit(solution)/shard_map/all_gather | solution.py:42
  11.9 39.9 %copy-start.5 = (s32[512]{0:T(512)S(1)}, s32[512]{0:T(512)}, u32[]{:S(2)}) copy-start(s32[512]{0:T(512)} %param.18) | copy-start | bytes 6148
  11.9 40.2 %copy-start.2 = (bf16[1,2048]{1,0:T(2,128)(2,1)S(1)}, bf16[1,2048]{1,0:T(2,128)(2,1)}, u32[]{:S(2)}) copy-start(bf16[1,2048]{1,0:T(2,128)(2,1)} %param.23) | copy-start | bytes 12292
  11.9 40.2 %copy-start.3 = (bf16[1,1024]{1,0:T(2,128)(2,1)S(1)}, bf16[1,1024]{1,0:T(2,128)(2,1)}, u32[]{:S(2)}) copy-start(bf16[1,1024]{1,0:T(2,128)(2,1)} %param.25) | copy-start | bytes 6148
  12.0 40.2 %copy-start.4 = (bf16[1,1024]{1,0:T(2,128)(2,1)S(1)}, bf16[1,1024]{1,0:T(2,128)(2,1)}, u32[]{:S(2)}) copy-start(bf16[1,1024]{1,0:T(2,128)(2,1)} %param.26) | copy-start | bytes 6148
  13.5 33.5 %all-to-all-start = ((bf16[32,1,16,1024]{3,2,1,0:T(8,128)(2,1)}), bf16[32,1,16,1024]{3,2,1,0:T(8,128)(2,1)S(1)}, u32[]{:S(2)}, u32[]{:S(2)}) async-start(bf16[32,1,16,1024]{3,2,1,0:T(8,128)(2,1)} %copy.75), calls=%async_computation | async-start | bytes 2097152 | tf_op jit(solution)/shard_map/all_to_all | solution.py:34
  47.0 26.8 %all-to-all-start.1 = ((bf16[32,1,16,1024]{3,2,1,0:T(8,128)(2,1)}), bf16[32,1,16,1024]{3,2,1,0:T(8,128)(2,1)S(1)}, u32[]{:S(2)}, u32[]{:S(2)}) async-start(bf16[32,1,16,1024]{3,2,1,0:T(8,128)(2,1)} %copy.76), calls=%async_computation.1 | async-start | bytes 2097152 | tf_op jit(solution)/shard_map/all_to_all | solution.py:34
  51.0 376.2 %all-gather.14.cloned.1.call-start = ((), (), s32[]{:S(2)}) async-start(), calls=%async_computation.3 | async-start | bytes 1572864 | tf_op jit(solution)/shard_map/all_gather | solution.py:62
  181.0 4.3 copy-start.1
  198.9 28.5 %collective-permute-start = (bf16[4,32,1024]{2,1,0:T(8,128)(2,1)S(1)}, bf16[4,32,1024]{2,1,0:T(8,128)(2,1)S(1)}, u32[]{:S(2)}, u32[]{:S(2)}) collective-permute-start(bf16[4,32,1024]{2,1,0:T(8,128)(2,1)S(1)} %bitcast.95), channel_id=1, source_target_pairs={{0,2},{2,0},{1,3},{3,1},{4,6},{6,4},{5,7},{7,5},{8,10},{10,8},{9,1... | collective-permute-start | bytes 786440 | tf_op jit(solution)/shard_map/while/body/eval_jaxpr/ppermute | solution.py:58
  266.3 4.2 collective-permute-start
  309.4 4.2 collective-permute-start
  352.5 4.2 collective-permute-start
  392.7 2.5 collective-permute-start
  410.8 4.7 %collective-permute-start = (bf16[4,32,1024]{2,1,0:T(8,128)(2,1)S(1)}, bf16[4,32,1024]{2,1,0:T(8,128)(2,1)S(1)}, u32[]{:S(2)}, u32[]{:S(2)}) collective-permute-start(bf16[4,32,1024]{2,1,0:T(8,128)(2,1)S(1)} %bitcast.95), channel_id=1, source_target_pairs={{0,2},{2,0},{1,3},{3,1},{4,6},{6,4},{5,7},{7,5},{8,10},{10,8},{9,1... | collective-permute-start | bytes 786440 | tf_op jit(solution)/shard_map/while/body/eval_jaxpr/ppermute | solution.py:58
Sparse Core Ops, SparseCore 0:
  10.5 154.2 all-gather.11
  417.6 9.5 all-gather.13
